TPU v7x, 32 devices: a whole 2x2x4 slice. The times are simulated.
32 devices in a mesh: groups: 2 (over x), seq: 16 (over z, y, core).
Axes of the slice: x: 2, y: 2, z: 4, core: 2. Of those that a mesh axis runs over, the one named last changes fastest.
Arguments:
- queries: bfloat16 [1024, 2048], P(('groups', 'seq')), parts along dimension 0, may hold values from -132 to 132
- fresh_keys: bfloat16 [1024, 2048], P(('groups', 'seq')), parts along dimension 0, may hold values from -6 to 6
- fresh_values: bfloat16 [1024, 2048], P(('groups', 'seq')), parts along dimension 0, may hold values from -48 to 48
- stale_keys: bfloat16 [1024, 2048], P(('groups', 'seq')), parts along dimension 0, may hold values from -6 to 6
- stale_values: bfloat16 [1024, 2048], P(('groups', 'seq')), parts along dimension 0, may hold values from -48 to 48
- patch_sizes: int32 [8], P('groups'), parts along dimension 0, may hold values from 1 to 256, 512 in all
Outputs:
- attended: bfloat16 [1024, 2048], P(('groups', 'seq')), parts along dimension 0
There are 2 independent parts, one for each index of `groups`. A program takes and returns all parts, laid end to end along the dimension named above; each array names one. Nothing has to cross between parts.
Inputs may be any that keep to these rules, and one draw needn't show every extreme that they name: `patch_sizes`: the patch lengths sum to 512.
All inputs are finite; a program needn't handle non-finite values.
Results may differ from a plain program's by a relative error of at most 0.006.
Values may be sent and summed in bfloat16 or wider, within the bound.
A program may use at most 64 MiB of HBM per device.

v0:
```python
import jax
import jax.numpy as jnp
from jax import lax
from jax.sharding import PartitionSpec as P

H = 16


def shifted(block, axis, distance):
    devices = range(lax.axis_size(axis))
    route = [((i - distance) % len(devices), i) for i in devices]
    return lax.ppermute(block, axis, route)


def shards(queries, fresh_keys, fresh_values, stale_keys, stale_values, patch_sizes):
    local_rows, columns = queries.shape
    head_size = columns // H
    devices = lax.axis_size("seq")
    query_groups = devices // H
    sub_rows = local_rows // query_groups
    shape_in = (sub_rows, devices, head_size)
    moved = (
        lax.all_to_all(queries.reshape(shape_in), "seq", split_axis=1, concat_axis=0, tiled=True),
        lax.all_to_all(
            fresh_keys.reshape(shape_in), "seq", split_axis=1, concat_axis=0, tiled=True
        ),
        lax.all_to_all(
            fresh_values.reshape(shape_in), "seq", split_axis=1, concat_axis=0, tiled=True
        ),
        lax.all_to_all(
            stale_keys.reshape(shape_in), "seq", split_axis=1, concat_axis=0, tiled=True
        ),
        lax.all_to_all(
            stale_values.reshape(shape_in), "seq", split_axis=1, concat_axis=0, tiled=True
        ),
    )
    query_rows = moved[0].reshape(-1, head_size)
    stacked = jnp.stack(
        [
            moved[1].reshape(-1, head_size),
            moved[2].reshape(-1, head_size),
            moved[3].reshape(-1, head_size),
            moved[4].reshape(-1, head_size),
        ]
    )
    own_group = lax.axis_index("seq") // H
    patch_ends = jnp.cumsum(patch_sizes)[:-1]
    positions = (
        jnp.arange(devices, dtype=jnp.int32)[:, None] * local_rows
        + jnp.arange(sub_rows, dtype=jnp.int32)[None, :] * query_groups
    ).reshape(-1)

    def patch_of(group):
        hits = positions[:, None] + group >= patch_ends[None, :]
        return jnp.sum(hits.astype(jnp.int32), axis=1)

    score_scale = head_size ** (-0.5)
    contract = (((1,), (1,)), ((), ()))
    query_patch = patch_of(own_group)

    def absorb(carry_state, key_block, source_group):
        running_max, denominator, numerator = carry_state
        is_fresh = patch_of(source_group)[None, :] <= query_patch[:, None]
        fresh_scores = lax.dot_general(
            query_rows, key_block[0], contract, preferred_element_type=jnp.float32
        )
        stale_scores = lax.dot_general(
            query_rows, key_block[2], contract, preferred_element_type=jnp.float32
        )
        scores = jnp.where(is_fresh, fresh_scores, stale_scores) * score_scale
        new_max = jnp.maximum(running_max, jnp.max(scores, axis=1, keepdims=True))
        rescale = jnp.exp(running_max - new_max)
        weights = jnp.exp(scores - new_max)
        denominator = denominator * rescale + jnp.sum(weights, axis=1, keepdims=True)
        rounded = weights.astype(jnp.bfloat16)
        zeroes = jnp.zeros_like(rounded)
        numerator = numerator * rescale + jnp.dot(
            jnp.where(is_fresh, rounded, zeroes), key_block[1], preferred_element_type=jnp.float32
        )
        numerator = numerator + jnp.dot(
            jnp.where(is_fresh, zeroes, rounded), key_block[3], preferred_element_type=jnp.float32
        )
        return (new_max, denominator, numerator)

    query_count = query_rows.shape[0]
    carry_state = (
        jnp.full((query_count, 1), -1e30, jnp.float32),
        jnp.zeros((query_count, 1), jnp.float32),
        jnp.zeros((query_count, head_size), jnp.float32),
    )
    carry_state = absorb(carry_state, stacked, own_group)
    travelling = stacked
    for offset in range(1, query_groups):
        travelling = shifted(travelling, "seq", H)
        carry_state = absorb(carry_state, travelling, (own_group - offset) % query_groups)
    attended = (carry_state[2] / carry_state[1]).astype(jnp.bfloat16)
    returned = lax.all_to_all(
        attended.reshape(devices, sub_rows, 1, head_size),
        "seq",
        split_axis=0,
        concat_axis=2,
        tiled=True,
    )
    return returned.reshape(local_rows, columns)


def solution(mesh):
    in_specs = (
        P(("groups", "seq"), None),
        P(("groups", "seq"), None),
        P(("groups", "seq"), None),
        P(("groups", "seq"), None),
        P(("groups", "seq"), None),
        P("groups"),
    )
    out_specs = P(("groups", "seq"), None)
    return jax.shard_map(shards, mesh=mesh, in_specs=in_specs, out_specs=out_specs, check_vma=False)
```

profile of v0, /device:TPU:0, one launch (start us, length us, event | category | flops | bytes accessed | tf_op | source)
XLA Modules:
  0.0 74.3 jit_solution(5553754712294257362)
XLA Ops:
  0.0 0.0 copy-start
  0.0 0.9 %copy-done = bf16[32,2048]{1,0:T(8,128)(2,1)S(1)} copy-done((bf16[32,2048]{1,0:T(8,128)(2,1)S(1)}, bf16[32,2048]{1,0:T(8,128)(2,1)}, u32[]{:S(2)}) %copy-start) | copy-done | bytes 131096
  0.9 0.7 copy_bitcast_fusion.5
  1.6 0.0 copy-start.1
  1.6 7.5 %all-to-all-start = ((bf16[32,16,128]{2,0,1:T(8,128)(2,1)}), bf16[32,16,128]{2,0,1:T(8,128)(2,1)S(1)}, u32[]{:S(2)}, u32[]{:S(2)}) async-start(bf16[32,16,128]{2,0,1:T(8,128)(2,1)} %copy_bitcast_fusion.5), calls=%async_computation | async-start | bytes 262144 | tf_op jit(solution)/shard_map/all_to_all | solution.py:23
  9.2 0.0 copy-start.5
  9.2 0.6 copy-done.5
  9.8 0.2 reduce-window.4
  10.0 0.0 copy-done.1
  10.0 0.0 copy-start.2
  10.0 0.7 copy_bitcast_fusion.4
  10.7 0.3 copy-done.2
  10.9 0.0 copy-start.3
  10.9 0.7 copy_bitcast_fusion.3
  11.6 0.1 add_add_fusion
  11.7 0.1 add.55
  11.8 0.1 copy-done.3
  11.9 0.7 copy_bitcast_fusion.2
  12.6 0.0 copy-start.4
  12.6 4.5 %all-to-all-done = bf16[32,16,128]{2,0,1:T(8,128)(2,1)S(1)} async-done(((bf16[32,16,128]{2,0,1:T(8,128)(2,1)}), bf16[32,16,128]{2,0,1:T(8,128)(2,1)S(1)}, u32[]{:S(2)}, u32[]{:S(2)}) %all-to-all-start) | async-done | bytes 131104 | tf_op jit(solution)/shard_map/all_to_all | solution.py:23
  17.0 3.5 %all-to-all-start.1 = ((bf16[32,16,128]{2,0,1:T(8,128)(2,1)}), bf16[32,16,128]{2,0,1:T(8,128)(2,1)S(1)}, u32[]{:S(2)}, u32[]{:S(2)}) async-start(bf16[32,16,128]{2,0,1:T(8,128)(2,1)} %copy_bitcast_fusion.4), calls=%async_computation.1 | async-start | bytes 262144 | tf_op jit(solution)/shard_map/all_to_all | solution.py:24
  20.6 0.1 convert_reduce_fusion
  20.6 0.0 copy-done.4
  20.6 0.7 copy_bitcast_fusion.1
  21.3 7.1 %all-to-all-done.1 = bf16[32,16,128]{2,0,1:T(8,128)(2,1)S(1)} async-done(((bf16[32,16,128]{2,0,1:T(8,128)(2,1)}), bf16[32,16,128]{2,0,1:T(8,128)(2,1)S(1)}, u32[]{:S(2)}, u32[]{:S(2)}) %all-to-all-start.1) | async-done | bytes 131104 | tf_op jit(solution)/shard_map/all_to_all | solution.py:24
  28.4 3.5 %all-to-all-start.2 = ((bf16[32,16,128]{2,0,1:T(8,128)(2,1)}), bf16[32,16,128]{2,0,1:T(8,128)(2,1)S(1)}, u32[]{:S(2)}, u32[]{:S(2)}) async-start(bf16[32,16,128]{2,0,1:T(8,128)(2,1)} %copy_bitcast_fusion.3), calls=%async_computation.2 | async-start | bytes 262144 | tf_op jit(solution)/shard_map/all_to_all | solution.py:30
  31.9 0.3 fusion.17
  32.2 7.6 %all-to-all-done.2 = bf16[32,16,128]{2,0,1:T(8,128)(2,1)S(1)} async-done(((bf16[32,16,128]{2,0,1:T(8,128)(2,1)}), bf16[32,16,128]{2,0,1:T(8,128)(2,1)S(1)}, u32[]{:S(2)}, u32[]{:S(2)}) %all-to-all-start.2) | async-done | bytes 131104 | tf_op jit(solution)/shard_map/all_to_all | solution.py:30
  39.8 3.5 %all-to-all-start.3 = ((bf16[32,16,128]{2,0,1:T(8,128)(2,1)}), bf16[32,16,128]{2,0,1:T(8,128)(2,1)S(1)}, u32[]{:S(2)}, u32[]{:S(2)}) async-start(bf16[32,16,128]{2,0,1:T(8,128)(2,1)} %copy_bitcast_fusion.2), calls=%async_computation.3 | async-start | bytes 262144 | tf_op jit(solution)/shard_map/all_to_all | solution.py:27
  43.3 0.3 fusion.16
  43.7 0.2 fusion.3
  43.9 7.3 %all-to-all-done.3 = bf16[32,16,128]{2,0,1:T(8,128)(2,1)S(1)} async-done(((bf16[32,16,128]{2,0,1:T(8,128)(2,1)}), bf16[32,16,128]{2,0,1:T(8,128)(2,1)S(1)}, u32[]{:S(2)}, u32[]{:S(2)}) %all-to-all-start.3) | async-done | bytes 131104 | tf_op jit(solution)/shard_map/all_to_all | solution.py:27
  51.2 3.5 %all-to-all-start.4 = ((bf16[32,16,128]{2,0,1:T(8,128)(2,1)}), bf16[32,16,128]{2,0,1:T(8,128)(2,1)S(1)}, u32[]{:S(2)}, u32[]{:S(2)}) async-start(bf16[32,16,128]{2,0,1:T(8,128)(2,1)} %copy_bitcast_fusion.1), calls=%async_computation.4 | async-start | bytes 262144 | tf_op jit(solution)/shard_map/all_to_all | solution.py:33
  54.7 0.4 convolution_add_fusion.1
  55.2 7.4 %all-to-all-done.4 = bf16[32,16,128]{2,0,1:T(8,128)(2,1)S(1)} async-done(((bf16[32,16,128]{2,0,1:T(8,128)(2,1)}), bf16[32,16,128]{2,0,1:T(8,128)(2,1)S(1)}, u32[]{:S(2)}, u32[]{:S(2)}) %all-to-all-start.4) | async-done | bytes 131104 | tf_op jit(solution)/shard_map/all_to_all | solution.py:33
  62.6 0.5 fusion.2
  63.1 10.5 %all_to_all.90 = bf16[16,32,1,128]{3,1,2,0:T(8,128)(2,1)S(1)} all-to-all(bf16[16,32,1,128]{3,1,2,0:T(8,128)(2,1)S(1)} %bitcast.79), channel_id=1, replica_groups=mesh['groups'=2,'seq'=16] {'seq'}, dimensions={0} | all-to-all | bytes 262144 | tf_op jit(solution)/shard_map/all_to_all | solution.py:97
  73.6 0.1 copy.34
  73.6 0.7 copy.47
  (4 shorter events, 0.0 us)
Async XLA Ops:
  0.0 0.9 %copy-start = (bf16[32,2048]{1,0:T(8,128)(2,1)S(1)}, bf16[32,2048]{1,0:T(8,128)(2,1)}, u32[]{:S(2)}) copy-start(bf16[32,2048]{1,0:T(8,128)(2,1)} %param.6) | copy-start | bytes 393220
  1.6 8.4 %copy-start.1 = (bf16[32,2048]{1,0:T(8,128)(2,1)S(1)}, bf16[32,2048]{1,0:T(8,128)(2,1)}, u32[]{:S(2)}) copy-start(bf16[32,2048]{1,0:T(8,128)(2,1)} %param.7) | copy-start | bytes 393220
  1.6 15.5 %all-to-all-start = ((bf16[32,16,128]{2,0,1:T(8,128)(2,1)}), bf16[32,16,128]{2,0,1:T(8,128)(2,1)S(1)}, u32[]{:S(2)}, u32[]{:S(2)}) async-start(bf16[32,16,128]{2,0,1:T(8,128)(2,1)} %copy_bitcast_fusion.5), calls=%async_computation | async-start | bytes 262144 | tf_op jit(solution)/shard_map/all_to_all | solution.py:23
  9.2 0.7 copy-start.5
  10.0 1.0 %copy-start.2 = (bf16[32,2048]{1,0:T(8,128)(2,1)S(1)}, bf16[32,2048]{1,0:T(8,128)(2,1)}, u32[]{:S(2)}) copy-start(bf16[32,2048]{1,0:T(8,128)(2,1)} %param.9) | copy-start | bytes 393220
  10.9 1.0 %copy-start.3 = (bf16[32,2048]{1,0:T(8,128)(2,1)S(1)}, bf16[32,2048]{1,0:T(8,128)(2,1)}, u32[]{:S(2)}) copy-start(bf16[32,2048]{1,0:T(8,128)(2,1)} %param.8) | copy-start | bytes 393220
  12.6 8.1 %copy-start.4 = (bf16[32,2048]{1,0:T(8,128)(2,1)S(1)}, bf16[32,2048]{1,0:T(8,128)(2,1)}, u32[]{:S(2)}) copy-start(bf16[32,2048]{1,0:T(8,128)(2,1)} %param.10) | copy-start | bytes 393220
  17.0 11.4 %all-to-all-start.1 = ((bf16[32,16,128]{2,0,1:T(8,128)(2,1)}), bf16[32,16,128]{2,0,1:T(8,128)(2,1)S(1)}, u32[]{:S(2)}, u32[]{:S(2)}) async-start(bf16[32,16,128]{2,0,1:T(8,128)(2,1)} %copy_bitcast_fusion.4), calls=%async_computation.1 | async-start | bytes 262144 | tf_op jit(solution)/shard_map/all_to_all | solution.py:24
  28.4 11.4 %all-to-all-start.2 = ((bf16[32,16,128]{2,0,1:T(8,128)(2,1)}), bf16[32,16,128]{2,0,1:T(8,128)(2,1)S(1)}, u32[]{:S(2)}, u32[]{:S(2)}) async-start(bf16[32,16,128]{2,0,1:T(8,128)(2,1)} %copy_bitcast_fusion.3), calls=%async_computation.2 | async-start | bytes 262144 | tf_op jit(solution)/shard_map/all_to_all | solution.py:30
  39.8 11.4 %all-to-all-start.3 = ((bf16[32,16,128]{2,0,1:T(8,128)(2,1)}), bf16[32,16,128]{2,0,1:T(8,128)(2,1)S(1)}, u32[]{:S(2)}, u32[]{:S(2)}) async-start(bf16[32,16,128]{2,0,1:T(8,128)(2,1)} %copy_bitcast_fusion.2), calls=%async_computation.3 | async-start | bytes 262144 | tf_op jit(solution)/shard_map/all_to_all | solution.py:27
  51.2 11.4 %all-to-all-start.4 = ((bf16[32,16,128]{2,0,1:T(8,128)(2,1)}), bf16[32,16,128]{2,0,1:T(8,128)(2,1)S(1)}, u32[]{:S(2)}, u32[]{:S(2)}) async-start(bf16[32,16,128]{2,0,1:T(8,128)(2,1)} %copy_bitcast_fusion.1), calls=%async_computation.4 | async-start | bytes 262144 | tf_op jit(solution)/shard_map/all_to_all | solution.py:33
where the time goes:
time: 74.9 us; the launch traced here: 74.3 us
  waiting for transfers between devices  33.9 us (45%)
  starting transfers between devices  21.6 us (29%)
  blocking collectives  10.5 us (14%)
  local copies, waits for them, and re-layouts  6.15 us (8%)
  matrix products  1.53 us (2%)
    all_to_all x1, blocking collectives, shards(): lax.all_to_all(attended.reshape(devices, sub_rows, 1, head_size), 'seq',...  10.5 us
    all_to_all x1, waiting for transfers between devices, shards(): lax.all_to_all(stale_keys.reshape(shape_in), 'seq', split_axis=1, concat_...  7.57 us
    all_to_all x1, starting transfers between devices, shards(): lax.all_to_all(queries.reshape(shape_in), 'seq', split_axis=1, concat_axi...  7.55 us
    all_to_all x1, waiting for transfers between devices, shards(): lax.all_to_all(stale_values.reshape(shape_in), 'seq', split_axis=1, conca...  7.43 us
    all_to_all x1, waiting for transfers between devices, shards(): lax.all_to_all(fresh_values.reshape(shape_in), 'seq', split_axis=1, conca...  7.33 us
    all_to_all x1, waiting for transfers between devices, shards(): lax.all_to_all(fresh_keys.reshape(shape_in), 'seq', split_axis=1, concat_...  7.11 us
    all_to_all x1, waiting for transfers between devices, shards(): lax.all_to_all(queries.reshape(shape_in), 'seq', split_axis=1, concat_axi...  4.46 us
    all_to_all x1, starting transfers between devices, shards(): lax.all_to_all(fresh_values.reshape(shape_in), 'seq', split_axis=1, conca...  3.51 us
  transfers between devices with their start and end apart: 5, of which 5 were waited for; matrix products, arithmetic and copies ran while one was open for 6% of the time, Pallas kernels for 0%

commit v1 on v0

--- a/solution.py
+++ b/solution.py
@@ -24,8 +24,14 @@
         lax.all_to_all(
             fresh_keys.reshape(shape_in), "seq", split_axis=1, concat_axis=0, tiled=True
         ),
-        lax.all_to_all(
-            fresh_values.reshape(shape_in), "seq", split_axis=1, concat_axis=0, tiled=True
+        jnp.concatenate(
+            lax.all_to_all(
+                jnp.stack(jnp.split(fresh_values.reshape(shape_in), lax.axis_size("seq"), axis=1)),
+                "seq",
+                0,
+                0,
+            ),
+            axis=0,
         ),
         lax.all_to_all(
             stale_keys.reshape(shape_in), "seq", split_axis=1, concat_axis=0, tiled=True

time: 74.9 us -> 82.2 us (1.097)
  local copies, waits for them, and re-layouts: 6.15 us -> 15.3 us
  waiting for transfers between devices: 33.9 us -> 29.5 us
  starting transfers between devices: 21.6 us -> 24.2 us
    unnamed x13 -> x29, local copies, waits for them, and re-layouts: 2.66 us -> 11.6 us
    all_to_all x1, waiting for transfers between devices: 4.46 us -> 0.01 us  [shards(): lax.all_to_all(queries.reshape(shape_in), 'seq', split_axis=1, concat_axi...]
    all_to_all x1, starting transfers between devices: 3.51 us -> 6.13 us  [shards(): lax.all_to_all(fresh_keys.reshape(shape_in), 'seq', split_axis=1, concat_...]
  transfers between devices with their start and end apart: 5 -> 5, of which waited for: 5 -> 4; matrix products, arithmetic and copies ran while one was open for 6% -> 17% of each run, Pallas kernels for 0% -> 0%
where the time goes in v1:
time: 82.2 us; the launch traced here: 81.7 us
  waiting for transfers between devices  29.5 us (36%)
  starting transfers between devices  24.2 us (29%)
  local copies, waits for them, and re-layouts  15.3 us (19%)
  blocking collectives  10.5 us (13%)
  matrix products  1.52 us (2%)
    unnamed x29, local copies, waits for them, and re-layouts  11.6 us
    all_to_all x1, blocking collectives, shards(): lax.all_to_all(attended.reshape(devices, sub_rows, 1, head_size), 'seq',...  10.5 us
    all_to_all x1, waiting for transfers between devices, shards(): lax.all_to_all(stale_keys.reshape(shape_in), 'seq', split_axis=1, concat_...  7.58 us
    all_to_all x1, starting transfers between devices, shards(): lax.all_to_all(queries.reshape(shape_in), 'seq', split_axis=1, concat_axi...  7.55 us
    all_to_all x1, waiting for transfers between devices, shards(): lax.all_to_all(stale_values.reshape(shape_in), 'seq', split_axis=1, conca...  7.43 us
    all_to_all x1, waiting for transfers between devices, shards(): lax.all_to_all(jnp.stack(jnp.split(fresh_values.reshape(shape_in), lax.ax...  7.33 us
    all_to_all x1, waiting for transfers between devices, shards(): lax.all_to_all(fresh_keys.reshape(shape_in), 'seq', split_axis=1, concat_...  7.14 us
    all_to_all x1, starting transfers between devices, shards(): lax.all_to_all(fresh_keys.reshape(shape_in), 'seq', split_axis=1, concat_...  6.13 us
  transfers between devices with their start and end apart: 5, of which 4 were waited for; matrix products, arithmetic and copies ran while one was open for 17% of the time, Pallas kernels for 0%

profile of v1, /device:TPU:0, one launch (start us, length us, event | category | flops | bytes accessed | tf_op | source)
XLA Modules:
  0.0 81.7 jit_solution(17580012997980046588)
XLA Ops:
  0.0 0.0 copy-start
  0.0 0.9 %copy-done = bf16[32,2048]{1,0:T(8,128)(2,1)S(1)} copy-done((bf16[32,2048]{1,0:T(8,128)(2,1)S(1)}, bf16[32,2048]{1,0:T(8,128)(2,1)}, u32[]{:S(2)}) %copy-start) | copy-done | bytes 131096
  0.9 0.7 copy_bitcast_fusion.4
  1.6 0.0 copy-start.1
  1.6 7.5 %all-to-all-start = ((bf16[32,16,128]{2,0,1:T(8,128)(2,1)}), bf16[32,16,128]{2,0,1:T(8,128)(2,1)S(1)}, u32[]{:S(2)}, u32[]{:S(2)}) async-start(bf16[32,16,128]{2,0,1:T(8,128)(2,1)} %copy_bitcast_fusion.4), calls=%async_computation | async-start | bytes 262144 | tf_op jit(solution)/shard_map/all_to_all | solution.py:23
  9.2 0.0 copy-start.5
  9.2 0.6 copy-done.5
  9.8 0.2 reduce-window.4
  10.0 0.0 copy-done.1
  10.0 0.0 copy-start.2
  10.0 0.7 copy_bitcast_fusion.3
  10.7 0.3 copy-done.2
  11.0 0.3 fusion.16
  11.2 0.6 constant_dynamic-update-slice_fusion.15
  11.9 0.1 add_add_fusion
  11.9 0.6 constant_dynamic-update-slice_fusion.14
  12.5 0.6 constant_dynamic-update-slice_fusion.13
  13.1 0.6 constant_dynamic-update-slice_fusion.12
  13.7 0.6 constant_dynamic-update-slice_fusion.11
  14.3 0.6 constant_dynamic-update-slice_fusion.10
  14.9 0.6 constant_dynamic-update-slice_fusion.9
  15.5 0.0 copy-start.3
  15.5 0.6 constant_dynamic-update-slice_fusion.8
  16.1 0.6 constant_dynamic-update-slice_fusion.7
  16.7 0.6 constant_dynamic-update-slice_fusion.6
  17.3 0.6 constant_dynamic-update-slice_fusion.5
  17.9 0.6 constant_dynamic-update-slice_fusion.4
  18.5 0.6 constant_dynamic-update-slice_fusion.3
  19.1 0.6 constant_dynamic-update-slice_fusion.2
  19.7 0.6 constant_dynamic-update-slice_fusion.1
  20.3 0.6 constant_dynamic-update-slice_fusion
  20.9 0.1 add.55
  21.0 0.0 copy-done.3
  21.0 0.7 copy_bitcast_fusion.2
  21.7 0.0 copy-start.4
  21.7 0.0 all-to-all-done
  21.7 6.1 %all-to-all-start.1 = ((bf16[32,16,128]{2,0,1:T(8,128)(2,1)}), bf16[32,16,128]{2,0,1:T(8,128)(2,1)S(1)}, u32[]{:S(2)}, u32[]{:S(2)}) async-start(bf16[32,16,128]{2,0,1:T(8,128)(2,1)} %copy_bitcast_fusion.3), calls=%async_computation.1 | async-start | bytes 262144 | tf_op jit(solution)/shard_map/all_to_all | solution.py:24
  27.9 0.1 convert_reduce_fusion
  27.9 0.0 copy-done.4
  27.9 0.7 copy_bitcast_fusion.1
  28.6 7.1 %all-to-all-done.1 = bf16[32,16,128]{2,0,1:T(8,128)(2,1)S(1)} async-done(((bf16[32,16,128]{2,0,1:T(8,128)(2,1)}), bf16[32,16,128]{2,0,1:T(8,128)(2,1)S(1)}, u32[]{:S(2)}, u32[]{:S(2)}) %all-to-all-start.1) | async-done | bytes 131104 | tf_op jit(solution)/shard_map/all_to_all | solution.py:24
  35.8 3.5 %all-to-all-start.2 = ((bf16[32,16,128]{2,0,1:T(8,128)(2,1)}), bf16[32,16,128]{2,0,1:T(8,128)(2,1)S(1)}, u32[]{:S(2)}, u32[]{:S(2)}) async-start(bf16[32,16,128]{2,0,1:T(8,128)(2,1)} %copy_bitcast_fusion.2), calls=%async_computation.2 | async-start | bytes 262144 | tf_op jit(solution)/shard_map/all_to_all | solution.py:36
  39.3 0.3 fusion.18
  39.6 7.6 %all-to-all-done.2 = bf16[32,16,128]{2,0,1:T(8,128)(2,1)S(1)} async-done(((bf16[32,16,128]{2,0,1:T(8,128)(2,1)}), bf16[32,16,128]{2,0,1:T(8,128)(2,1)S(1)}, u32[]{:S(2)}, u32[]{:S(2)}) %all-to-all-start.2) | async-done | bytes 131104 | tf_op jit(solution)/shard_map/all_to_all | solution.py:36
  47.1 3.5 %all-to-all-start.3 = ((bf16[16,32,1,128]{3,1,2,0:T(8,128)(2,1)}), bf16[16,32,1,128]{3,1,2,0:T(8,128)(2,1)S(1)}, u32[]{:S(2)}, u32[]{:S(2)}) async-start(bf16[16,32,1,128]{3,1,2,0:T(8,128)(2,1)} %constant_dynamic-update-slice_fusion), calls=%async_computation.3 | async-start | bytes 262144 | tf_op jit(solution)/shard_map/all_to_all | solution.py:28
  50.7 0.3 fusion.17
  51.0 0.2 fusion.3
  51.2 7.3 %all-to-all-done.3 = bf16[16,32,1,128]{3,1,2,0:T(8,128)(2,1)S(1)} async-done(((bf16[16,32,1,128]{3,1,2,0:T(8,128)(2,1)}), bf16[16,32,1,128]{3,1,2,0:T(8,128)(2,1)S(1)}, u32[]{:S(2)}, u32[]{:S(2)}) %all-to-all-start.3) | async-done | bytes 131104 | tf_op jit(solution)/shard_map/all_to_all | solution.py:28
  58.5 3.5 %all-to-all-start.4 = ((bf16[32,16,128]{2,0,1:T(8,128)(2,1)}), bf16[32,16,128]{2,0,1:T(8,128)(2,1)S(1)}, u32[]{:S(2)}, u32[]{:S(2)}) async-start(bf16[32,16,128]{2,0,1:T(8,128)(2,1)} %copy_bitcast_fusion.1), calls=%async_computation.4 | async-start | bytes 262144 | tf_op jit(solution)/shard_map/all_to_all | solution.py:39
  62.1 0.4 convolution_add_fusion.1
  62.5 7.4 %all-to-all-done.4 = bf16[32,16,128]{2,0,1:T(8,128)(2,1)S(1)} async-done(((bf16[32,16,128]{2,0,1:T(8,128)(2,1)}), bf16[32,16,128]{2,0,1:T(8,128)(2,1)S(1)}, u32[]{:S(2)}, u32[]{:S(2)}) %all-to-all-start.4) | async-done | bytes 131104 | tf_op jit(solution)/shard_map/all_to_all | solution.py:39
  69.9 0.5 fusion.2
  70.4 10.5 %all_to_all.80 = bf16[16,32,1,128]{3,1,2,0:T(8,128)(2,1)S(1)} all-to-all(bf16[16,32,1,128]{3,1,2,0:T(8,128)(2,1)S(1)} %bitcast.106), channel_id=1, replica_groups=mesh['groups'=2,'seq'=16] {'seq'}, dimensions={0} | all-to-all | bytes 262144 | tf_op jit(solution)/shard_map/all_to_all | solution.py:103
  80.9 0.1 copy.225
  81.0 0.7 copy.269
  (5 shorter events, 0.0 us)
Async XLA Ops:
  0.0 0.9 %copy-start = (bf16[32,2048]{1,0:T(8,128)(2,1)S(1)}, bf16[32,2048]{1,0:T(8,128)(2,1)}, u32[]{:S(2)}) copy-start(bf16[32,2048]{1,0:T(8,128)(2,1)} %param.6) | copy-start | bytes 393220
  1.6 8.4 %copy-start.1 = (bf16[32,2048]{1,0:T(8,128)(2,1)S(1)}, bf16[32,2048]{1,0:T(8,128)(2,1)}, u32[]{:S(2)}) copy-start(bf16[32,2048]{1,0:T(8,128)(2,1)} %param.7) | copy-start | bytes 393220
  1.6 20.1 %all-to-all-start = ((bf16[32,16,128]{2,0,1:T(8,128)(2,1)}), bf16[32,16,128]{2,0,1:T(8,128)(2,1)S(1)}, u32[]{:S(2)}, u32[]{:S(2)}) async-start(bf16[32,16,128]{2,0,1:T(8,128)(2,1)} %copy_bitcast_fusion.4), calls=%async_computation | async-start | bytes 262144 | tf_op jit(solution)/shard_map/all_to_all | solution.py:23
  9.2 0.7 copy-start.5
  10.0 1.0 %copy-start.2 = (bf16[32,2048]{1,0:T(8,128)(2,1)S(1)}, bf16[32,2048]{1,0:T(8,128)(2,1)}, u32[]{:S(2)}) copy-start(bf16[32,2048]{1,0:T(8,128)(2,1)} %param.8) | copy-start | bytes 393220
  15.5 5.5 %copy-start.3 = (bf16[32,2048]{1,0:T(8,128)(2,1)S(1)}, bf16[32,2048]{1,0:T(8,128)(2,1)}, u32[]{:S(2)}) copy-start(bf16[32,2048]{1,0:T(8,128)(2,1)} %param.9) | copy-start | bytes 393220
  21.7 6.2 %copy-start.4 = (bf16[32,2048]{1,0:T(8,128)(2,1)S(1)}, bf16[32,2048]{1,0:T(8,128)(2,1)}, u32[]{:S(2)}) copy-start(bf16[32,2048]{1,0:T(8,128)(2,1)} %param.10) | copy-start | bytes 393220
  21.7 14.0 %all-to-all-start.1 = ((bf16[32,16,128]{2,0,1:T(8,128)(2,1)}), bf16[32,16,128]{2,0,1:T(8,128)(2,1)S(1)}, u32[]{:S(2)}, u32[]{:S(2)}) async-start(bf16[32,16,128]{2,0,1:T(8,128)(2,1)} %copy_bitcast_fusion.3), calls=%async_computation.1 | async-start | bytes 262144 | tf_op jit(solution)/shard_map/all_to_all | solution.py:24
  35.8 11.4 %all-to-all-start.2 = ((bf16[32,16,128]{2,0,1:T(8,128)(2,1)}), bf16[32,16,128]{2,0,1:T(8,128)(2,1)S(1)}, u32[]{:S(2)}, u32[]{:S(2)}) async-start(bf16[32,16,128]{2,0,1:T(8,128)(2,1)} %copy_bitcast_fusion.2), calls=%async_computation.2 | async-start | bytes 262144 | tf_op jit(solution)/shard_map/all_to_all | solution.py:36
  47.1 11.4 %all-to-all-start.3 = ((bf16[16,32,1,128]{3,1,2,0:T(8,128)(2,1)}), bf16[16,32,1,128]{3,1,2,0:T(8,128)(2,1)S(1)}, u32[]{:S(2)}, u32[]{:S(2)}) async-start(bf16[16,32,1,128]{3,1,2,0:T(8,128)(2,1)} %constant_dynamic-update-slice_fusion), calls=%async_computation.3 | async-start | bytes 262144 | tf_op jit(solution)/shard_map/all_to_all | solution.py:28
  58.5 11.4 %all-to-all-start.4 = ((bf16[32,16,128]{2,0,1:T(8,128)(2,1)}), bf16[32,16,128]{2,0,1:T(8,128)(2,1)S(1)}, u32[]{:S(2)}, u32[]{:S(2)}) async-start(bf16[32,16,128]{2,0,1:T(8,128)(2,1)} %copy_bitcast_fusion.1), calls=%async_computation.4 | async-start | bytes 262144 | tf_op jit(solution)/shard_map/all_to_all | solution.py:39
